TPU v7x, 256 devices: a whole 4x4x8 slice. The times are simulated.
256 devices in a mesh: tm: 8 (over x, core), space: 32 (over y, z).
Axes of the slice: x: 4, y: 4, z: 8, core: 2. Of those that a mesh axis runs over, the one named last changes fastest.
Arguments:
- water_depth: float32 [96, 16, 128], P('space'), may hold values from 0.7 to 1.4
- momentum: float32 [96, 2, 16, 128], P('space'), may hold values from -0.6 to 0.6
- slot_live: int32 [96], P('space'), may hold values from 0 to 1, as said below
- neighbours: int32 [96, 2], P('space'), may hold values from 0 to 3, as said below
Outputs:
- slice_ends: float32 [8, 96, 3, 16, 128], P('tm', 'space')
Inputs may be any that keep to these rules, and one draw needn't show every extreme that they name: `slot_live`: every owner's 3 consecutive slots hold between 1 and 3 live blocks; owners 2p and 2p + 1 together hold exactly 4 live blocks, and some owner holds 3. `neighbours`: the live blocks of each owner form one run along the channel, and the runs of owners 0, 1, 2 and so on follow one another around the periodic channel. For a live slot, entry 0 names the slot of the same owner holding the block to the west and entry 1 the one to the east, or 3 where that block belongs to the previous (west) or next (east) owner; each owner has exactly one live slot with entry 0 equal to 3 and one with entry 1 equal to 3. A dead slot names itself in both entries.
All inputs are finite; a program needn't handle non-finite values.
Results may differ from a plain program's by a relative error of at most 0.00002.
Values sent between devices are 32-bit elements; how exact they have to be, the bound alone decides.
A program may use at most 64 MiB of HBM per device.

v0:
```python
import functools

import jax
import jax.numpy as jnp
from jax import lax
from jax.experimental import pallas as pl
from jax.experimental.pallas import tpu as pltpu
from jax.sharding import PartitionSpec as P

SUB = 3
TIME_STEP = 0.15
ROWS = 16
HALF = 8
LANES = 128
SLICES_REACH = 24
VMEM_LIMIT = 60 * 1024 * 1024
MESH = pl.DeviceIdType.MESH


def pick(index, values):
    result = values[-1]
    for i in range(len(values) - 2, -1, -1):
        result = jnp.where(index == i, values[i], result)
    return result


def derived(h, m, n):
    r = lax.rsqrt(h)
    c = h * r
    inv = r * r
    u = m * inv
    q = n * inv
    p = 0.5 * h * h
    f1 = m * u + p
    f2 = n * u
    g2 = n * q + p
    sx = jnp.abs(u) + c
    sy = jnp.abs(q) + c
    return f1, f2, g2, sx, sy


def faces(a_v, b_v, a_f, b_f, a_s, b_s):
    top = jnp.maximum(a_s, b_s)
    return [(fa + fb) - top * (vb - va) for va, vb, fa, fb in zip(a_v, b_v, a_f, b_f)]


def shift(x, distance):
    return pltpu.roll(x, (-distance) % LANES, 1)


def rows_part(v, d, row):
    n = v[2]
    f1, f2, g2, sx, sy = d
    up = lambda x: pltpu.roll(x, HALF - 1, 0)
    down = lambda x: pltpu.roll(x, 1, 0)
    vn = [up(x) for x in v]
    wy = faces(v, vn, (n, f2, g2), (vn[2], up(f2), up(g2)), sy, up(sy))
    last, first = row == HALF - 1, row == 0
    sn = sy * n
    zero = jnp.zeros_like(n)
    high = [jnp.where(last, w, x) for w, x in zip((zero, zero, 2.0 * (g2 + sn)), wy)]
    low = [jnp.where(first, w, down(x)) for w, x in zip((zero, zero, 2.0 * (g2 - sn)), wy)]
    return [(-0.5 * TIME_STEP) * (x - y) for x, y in zip(high, low)]


def lane_face(v0, d0, v1, d1):
    return faces(v0, v1, (v0[1], d0[0], d0[1]), (v1[1], d1[0], d1[1]), d0[3], d1[3])


def coarse(v, row):
    a = -0.5 * TIME_STEP * SUB
    at = {o: [shift(x, o) if o else x for x in v] for o in (0, 1, -1, 2, -2)}
    d = {0: derived(*at[0])}
    across = {0: rows_part(at[0], d[0], row)}
    for o in (1, -1):
        across[o] = [shift(y, o) for y in across[0]]
    for o in (1, -1, 2, -2):
        d[o] = derived(*at[o])
    w = {o: lane_face(at[o], d[o], at[o + 1], d[o + 1]) for o in (0, -1, 1, -2)}
    v1 = {
        o: [x + (a * (r - l) + y) for x, r, l, y in zip(at[o], w[o], w[o - 1], across[o])]
        for o in (0, 1, -1)
    }
    e = {o: derived(*v1[o]) for o in (0, 1, -1)}
    across1 = rows_part(v1[0], e[0], row)
    w1 = {o: lane_face(v1[o], e[o], v1[o + 1], e[o + 1]) for o in (0, -1)}
    return [
        0.5 * ((x + x1) + (a * (r - l) + y))
        for x, x1, r, l, y in zip(v, v1[0], w1[0], w1[-1], across1)
    ]


def fine_pass(load, emit, ahead=2):
    v, d, e, w = {}, {}, {}, {}
    low = None
    for t in range(ROWS + 2 * ahead):
        if t < ROWS:
            v[t] = load(t)
            d[t] = derived(*v[t])
            e[t] = [shift(x, 1) for x in (*v[t], d[t][0], d[t][1], d[t][3])]
        j = t - ahead
        if 0 <= j < ROWS:
            f1, f2, g2, sx, sy = d[j]
            x = e[j]
            wx = faces(v[j], x[:3], (v[j][1], f1, f2), (x[1], x[3], x[4]), sx, x[5])
            w[j] = (wx, [shift(y, -1) for y in wx])
        j = t - 2 * ahead
        if 0 <= j < ROWS:
            h, m, n = v[j]
            f1, f2, g2, sx, sy = d[j]
            if j == 0:
                low = [None, None, 2.0 * (g2 - sy * n)]
            if j + 1 < ROWS:
                f1a, f2a, g2a, sxa, sya = d[j + 1]
                high = faces(v[j], v[j + 1], (n, f2, g2), (v[j + 1][2], f2a, g2a), sy, sya)
            else:
                high = [None, None, 2.0 * (g2 + sy * n)]
            diff = []
            for right, left, hi, lo in zip(*w[j], high, low):
                y = right - left
                if hi is not None:
                    y = y + hi
                if lo is not None:
                    y = y - lo
                diff.append(y)
            emit(j, v[j], diff)
            low = high


def fine(state, mid):
    def at(ref, j):
        return [ref[f, HALF * j : HALF * j + HALF, :] for f in range(3)]

    def put(ref, j, v):
        for f in range(3):
            ref[f, HALF * j : HALF * j + HALF, :] = v[f]

    def first(j, v, d):
        put(mid, j, [x - (0.5 * TIME_STEP) * y for x, y in zip(v, d)])

    def second(j, v1, d):
        v = at(state, j)
        put(state, j, [0.5 * (x + y) - (0.25 * TIME_STEP) * z for x, y, z in zip(v, v1, d)])

    def once(i, run):
        def trip(_, carry):
            run()
            return carry

        lax.fori_loop(0, jnp.minimum(i, 0) + 1, trip, 0)

    def step(i, carry):
        once(i, lambda: fine_pass(lambda j: at(state, j), first))
        once(i, lambda: fine_pass(lambda j: at(mid, j), second))
        return carry

    lax.fori_loop(0, SUB, step, 0)


def seams(n_tm, blocks, seg):
    reach = SLICES_REACH
    west = [n for n in range(n_tm) if seg * n - reach < 0]
    east = [
        n
        for n in range(n_tm)
        if any(seg * n < LANES * k < seg * n + seg + reach for k in range(1, blocks + 1))
    ]
    assert not set(west) & set(east)
    return west, east


def member(me, places):
    return functools.reduce(jnp.logical_or, [me == n for n in places])


def tables(live_ref, nb_ref, blocks):
    lives = [live_ref[b] == 1 for b in range(blocks)]
    count = jnp.int32(0)
    first = jnp.int32(0)
    final = jnp.int32(0)
    for b in range(blocks):
        count = count + jnp.where(lives[b], 1, 0)
        first = first + jnp.where(jnp.logical_and(lives[b], nb_ref[0, b] == blocks), b, 0)
        final = final + jnp.where(jnp.logical_and(lives[b], nb_ref[1, b] == blocks), b, 0)
    easts = [nb_ref[1, b] for b in range(blocks)]
    order = [first]
    for _ in range(blocks - 1):
        order.append(jnp.minimum(pick(order[-1], easts), blocks - 1))
    return lives, count, final, order


def window_kernel(
    n_tm, owners, seg,
    live_hbm, nb_hbm, depth_ref, mom_ref, win_ref,
    loc, edge, got, live_ref, nb_ref,
    in_sem, edge_send, edge_recv,
):
    me = lax.axis_index("tm")
    own = lax.axis_index("space")
    east_owner = lax.rem(own + 1, owners)
    west_owner = lax.rem(own + owners - 1, owners)
    blocks = loc.shape[0]
    west_set, east_set = seams(n_tm, blocks, seg)
    at_west, at_east = member(me, west_set), member(me, east_set)
    at_seam = jnp.logical_or(at_west, at_east)

    copies = [
        pltpu.make_async_copy(nb_hbm, nb_ref, in_sem.at[0]),
        pltpu.make_async_copy(live_hbm, live_ref, in_sem.at[1]),
        pltpu.make_async_copy(depth_ref, loc.at[:, 0], in_sem.at[2]),
        pltpu.make_async_copy(mom_ref, loc.at[:, 1:3], in_sem.at[3]),
    ]
    for c in copies:
        c.start()
    barrier = pltpu.get_barrier_semaphore()

    @pl.when(at_seam)
    def _():
        for o in (west_owner, east_owner):
            pl.semaphore_signal(barrier, inc=1, device_id=(me, o), device_id_type=MESH)

    for c in copies:
        c.wait()
    lives, count, final, order = tables(live_ref, nb_ref, blocks)

    halo = pltpu.make_async_remote_copy(
        src_ref=edge, dst_ref=got, send_sem=edge_send, recv_sem=edge_recv,
        device_id=(me, jnp.where(at_west, east_owner, west_owner)), device_id_type=MESH,
    )
    edge[...] = loc[jnp.where(at_west, final, order[0])]

    @pl.when(at_seam)
    def _():
        pl.semaphore_wait(barrier, 2)
        halo.start()

    pad = (LANES - seg) // 2
    begin = seg * me + (LANES - pad)
    place = begin // LANES - 1
    offset = begin % LANES
    lane = lax.broadcasted_iota(jnp.int32, (3, ROWS, LANES), 2)
    left = lane >= offset

    def slot(position):
        return jnp.clip(pick(position, order), 0, blocks - 1)

    win_ref[...] = jnp.where(left, loc[slot(place)], loc[slot(place + 1)])

    @pl.when(at_seam)
    def _():
        halo.wait()
        outside_a = jnp.logical_or(place < 0, place >= count)
        outside_b = place + 1 >= count
        mask = jnp.logical_or(
            jnp.logical_and(left, outside_a), jnp.logical_and(jnp.logical_not(left), outside_b)
        )
        win_ref[...] = jnp.where(mask, got[...], win_ref[...])


def main_kernel(
    n_tm, seg,
    live_hbm, nb_hbm, win_ref, out_ref,
    state, mid, delta, ga, ka, send, recv, run, live_ref, nb_ref,
    in_sem, tm_send, tm_recv,
):
    me = lax.axis_index("tm")
    own = lax.axis_index("space")
    blocks = out_ref.shape[1]
    copies = [
        pltpu.make_async_copy(nb_hbm, nb_ref, in_sem.at[0]),
        pltpu.make_async_copy(live_hbm, live_ref, in_sem.at[1]),
    ]
    for c in copies:
        c.start()
    barrier = pltpu.get_barrier_semaphore()
    for d in range(1, n_tm):
        peer = lax.rem(me + d, n_tm)
        pl.semaphore_signal(barrier, inc=1, device_id=(peer, own), device_id_type=MESH)

    row = lax.broadcasted_iota(jnp.int32, (HALF, LANES), 0)
    for f in range(3):
        for half in range(2):
            rows = win_ref[f, pl.ds(HALF * half, HALF), :]
            for m in (0, n_tm - 1):
                state[f, pl.ds(64 * half + m, HALF, stride=8), :] = rows

    def pair(f, m):
        return state[f, pl.ds(m, HALF, stride=16), :], state[f, pl.ds(m + 8, HALF, stride=16), :]

    def mean(m):
        out = []
        for f in range(3):
            a, b = pair(f, m)
            out.append(0.5 * (a + b))
        return out

    def chain0(n, c):
        g = coarse(c, row)
        for f in range(3):
            ga[n, f] = g[f]
            state[f, pl.ds(n + 1, HALF, stride=16), :] = g[f]
            state[f, pl.ds(n + 9, HALF, stride=16), :] = g[f]
        return g

    c6 = lax.fori_loop(0, n_tm - 2, chain0, mean(0))

    fine(state, mid)

    def deliver(n, even, odd):
        for f in range(3):
            send[n, f, pl.ds(0, HALF, stride=2), :] = even[f]
            send[n, f, pl.ds(1, HALF, stride=2), :] = odd[f]

    def message(n):
        return pltpu.make_async_remote_copy(
            src_ref=send.at[n], dst_ref=recv.at[me], send_sem=tm_send.at[n], recv_sem=tm_recv.at[me],
            device_id=(n, own), device_id_type=MESH,
        )

    def dispatch(n):
        @pl.when(n != me)
        def _():
            message(n).start()

    pairs = [pair(f, 0) for f in range(3)]
    deliver(0, [a for a, _ in pairs], [b for _, b in pairs])
    pl.semaphore_wait(barrier, n_tm - 1)
    dispatch(0)
    for f in range(3):
        for m in (0, n_tm - 1):
            delta[f, pl.ds(m, HALF, stride=8), :] = jnp.zeros((HALF, LANES), jnp.float32)

    def keep1(n, k, g):
        out = []
        for f in range(3):
            ka[n, f] = k[f]
            a, b = pair(f, n)
            d = k[f] - g[f]
            delta[f, pl.ds(n, HALF, stride=8), :] = d
            out.append(d + 0.5 * (a + b))
        return out

    k1, g6 = coarse(mean(0), row), coarse(c6, row)
    for f in range(3):
        ga[n_tm - 2, f] = g6[f]
    c = keep1(1, k1, [ga[1, f] for f in range(3)])

    def chain1(n, c):
        return keep1(n, coarse(c, row), [ga[n, f] for f in range(3)])

    c7 = lax.fori_loop(2, n_tm - 1, chain1, c)
    for f in range(3):
        for j in range(HALF):
            d = delta[f, HALF * j : HALF * j + HALF, :]
            for i in (2 * j, 2 * j + 1):
                state[f, HALF * i : HALF * i + HALF, :] = state[f, HALF * i : HALF * i + HALF, :] + d

    fine(state, mid)
    pairs = [pair(f, 0) for f in range(3)]
    deliver(1, [a for a, _ in pairs], [b for _, b in pairs])
    dispatch(1)

    def keep2(n, k):
        even, odd, out = [], [], []
        for f in range(3):
            a, b = pair(f, n - 1)
            d = k[f] - ka[n, f]
            even.append(a + d)
            odd.append(b + d)
            out.append(d + 0.5 * (a + b))
        deliver(n, even, odd)
        dispatch(n)
        return out

    k2, k7 = coarse(mean(0), row), coarse(c7, row)
    for f in range(3):
        ka[n_tm - 1, f] = k7[f]
    lax.fori_loop(3, n_tm, lambda n, c: keep2(n, coarse(c, row)), keep2(2, k2))

    recv[me] = send[me]
    for c in copies:
        c.wait()
    lives, count, _, order = tables(live_ref, nb_ref, blocks)
    for p in range(n_tm):
        @pl.when(p != me)
        def _():
            pltpu.make_async_remote_copy(
                src_ref=send.at[p], dst_ref=recv.at[p], send_sem=tm_send.at[p], recv_sem=tm_recv.at[p],
                device_id=(p, own), device_id_type=MESH,
            ).wait()

    lane = lax.broadcasted_iota(jnp.int32, (HALF, LANES), 1)
    for b in range(blocks):
        lo = LANES * b
        parts = [p for p in range(n_tm) if seg * p < lo + LANES and seg * p + seg > lo]
        for f in range(3):
            for half in range(2):
                rows = pl.ds(HALF * half, HALF)
                value = recv[parts[0], f, rows, :]
                for p in parts[1:]:
                    value = jnp.where(lane >= seg * p - lo, recv[p, f, rows, :], value)
                run[b, f, rows, :] = value
    for b in range(blocks):
        spot = jnp.int32(0)
        for i in range(1, blocks):
            spot = jnp.where(jnp.logical_and(order[i] == b, count > i), i, spot)
        out_ref[0, b] = jnp.where(lives[b], run[spot], 0.0)


def solution(mesh):
    n_tm, owners = mesh.shape["tm"], mesh.shape["space"]
    blocks = 3
    seg = blocks * LANES // n_tm
    f32, i32 = jnp.float32, jnp.int32
    dma = pltpu.SemaphoreType.DMA
    hbm = pl.BlockSpec(memory_space=pltpu.HBM)
    vmem = pl.BlockSpec(memory_space=pltpu.VMEM)
    small = [pltpu.SMEM((blocks,), i32), pltpu.SMEM((2, blocks), i32)]

    def local(water_depth, momentum, slot_live, neighbours):
        sides = neighbours.T
        window = pl.pallas_call(
            functools.partial(window_kernel, n_tm, owners, seg),
            out_shape=pltpu.VMEM((3, ROWS, LANES), f32),
            in_specs=[hbm] * 4,
            out_specs=vmem,
            scratch_shapes=[
                pltpu.VMEM((blocks, 3, ROWS, LANES), f32),
                pltpu.VMEM((3, ROWS, LANES), f32),
                pltpu.VMEM((3, ROWS, LANES), f32),
                *small,
                dma((4,)),
                dma,
                dma,
            ],
            compiler_params=pltpu.CompilerParams(collective_id=0, has_side_effects=True, vmem_limit_bytes=VMEM_LIMIT),
            name="window",
        )(slot_live, sides, water_depth, momentum)
        return pl.pallas_call(
            functools.partial(main_kernel, n_tm, seg),
            out_shape=pltpu.VMEM((1, blocks, 3, ROWS, LANES), f32),
            in_specs=[hbm, hbm, vmem],
            out_specs=vmem,
            scratch_shapes=[
                pltpu.VMEM((3, HALF * ROWS, LANES), f32),
                pltpu.VMEM((3, HALF * ROWS, LANES), f32),
                pltpu.VMEM((3, HALF * HALF, LANES), f32),
                pltpu.VMEM((n_tm, 3, HALF, LANES), f32),
                pltpu.VMEM((n_tm, 3, HALF, LANES), f32),
                pltpu.VMEM((n_tm, 3, ROWS, LANES), f32),
                pltpu.VMEM((n_tm, 3, ROWS, LANES), f32),
                pltpu.VMEM((blocks, 3, ROWS, LANES), f32),
                *small,
                dma((2,)),
                dma((n_tm,)),
                dma((n_tm,)),
            ],
            compiler_params=pltpu.CompilerParams(collective_id=1, has_side_effects=True, vmem_limit_bytes=VMEM_LIMIT),
            name="parareal",
        )(slot_live, sides, pltpu.with_memory_space_constraint(window, pltpu.VMEM))

    return jax.shard_map(
        local,
        mesh=mesh,
        in_specs=(P("space", None, None), P("space", None, None, None), P("space"), P("space", None)),
        out_specs=P("tm", "space", None, None, None),
        check_vma=False,
    )
```

profile of v0, /device:TPU:1, one launch (start us, length us, event | category | flops | bytes accessed | tf_op | source)
XLA Modules:
  0.0 21.7 jit_solution(756898054822775921)
XLA Ops:
  0.0 0.9 %window.1.win_ref = f32[3,16,128]{2,1,0:T(8,128)S(1)} custom-call(s32[3]{0:T(128)} %live_hbm.3, s32[2,3]{1,0:T(2,128)} %bitcast.1, f32[3,16,128]{2,1,0:T(8,128)} %depth_ref.1, f32[3,2,16,128]{3,2,1,0:T(8,128)} %mom_ref.1), custom_call_target="tpu_custom_call" | custom-call | tf_op jit(solution)/shard_map/window/pallas_call | solution.py:422
  0.9 20.2 %parareal.1 = f32[1,3,3,16,128]{4,3,2,1,0:T(8,128)S(1)} custom-call(s32[3]{0:T(128)} %live_hbm.3, s32[2,3]{1,0:T(2,128)} %bitcast.2, f32[3,16,128]{2,1,0:T(8,128)S(1)} %window.1.win_ref), custom_call_target="tpu_custom_call" | custom-call | tf_op jit(solution)/shard_map/parareal/pallas_call | solution.py:439
  21.0 0.6 %copy.6 = f32[1,3,3,16,128]{4,3,2,1,0:T(8,128)} copy(f32[1,3,3,16,128]{4,3,2,1,0:T(8,128)S(1)} %parareal.1) | data formatting | bytes 147456
where the time goes:
time: 21.8 us; the launch traced here: 21.7 us
  Pallas kernels  21 us (96%)
  local copies, waits for them, and re-layouts  0.64 us (3%)
    pallas_call x1, Pallas kernels, local(): pl.pallas_call(functools.partial(main_kernel, n_tm, seg), out_shape=pltpu...  20.2 us
    pallas_call x1, Pallas kernels, local(): pl.pallas_call(functools.partial(window_kernel, n_tm, owners, seg), out_s...  0.88 us
    unnamed x1, local copies, waits for them, and re-layouts  0.64 us

commit v1 on v0

--- a/solution.py
+++ b/solution.py
@@ -12,7 +12,9 @@
 ROWS = 16
 HALF = 8
 LANES = 128
-SLICES_REACH = 24
+REACH = 24
+STARTS = (0, 48, 96, 144, 192, 232, 288, 336, 384)
+HOLDS = (1, 0, 3, 2, 4, 7, 6, 5)
 VMEM_LIMIT = 60 * 1024 * 1024
 MESH = pl.DeviceIdType.MESH
 
@@ -157,15 +159,16 @@
     lax.fori_loop(0, SUB, step, 0)
 
 
-def seams(n_tm, blocks, seg):
-    reach = SLICES_REACH
-    west = [n for n in range(n_tm) if seg * n - reach < 0]
+def seams(blocks):
+    spans = [(STARTS[k], STARTS[k + 1]) for k in HOLDS]
+    west = [n for n, (lo, _) in enumerate(spans) if lo < REACH]
     east = [
         n
-        for n in range(n_tm)
-        if any(seg * n < LANES * k < seg * n + seg + reach for k in range(1, blocks + 1))
+        for n, (lo, hi) in enumerate(spans)
+        if any(lo < LANES * k < hi + REACH for k in range(1, blocks + 1))
     ]
     assert not set(west) & set(east)
+    assert max(hi - lo for lo, hi in spans) + 2 * REACH <= LANES
     return west, east
 
 
@@ -190,7 +193,7 @@
 
 
 def window_kernel(
-    n_tm, owners, seg,
+    owners,
     live_hbm, nb_hbm, depth_ref, mom_ref, win_ref,
     loc, edge, got, live_ref, nb_ref,
     in_sem, edge_send, edge_recv,
@@ -200,7 +203,7 @@
     east_owner = lax.rem(own + 1, owners)
     west_owner = lax.rem(own + owners - 1, owners)
     blocks = loc.shape[0]
-    west_set, east_set = seams(n_tm, blocks, seg)
+    west_set, east_set = seams(blocks)
     at_west, at_east = member(me, west_set), member(me, east_set)
     at_seam = jnp.logical_or(at_west, at_east)
 
@@ -234,10 +237,9 @@
         pl.semaphore_wait(barrier, 2)
         halo.start()
 
-    pad = (LANES - seg) // 2
-    begin = seg * me + (LANES - pad)
-    place = begin // LANES - 1
-    offset = begin % LANES
+    begins = [STARTS[k] - (LANES - STARTS[k + 1] + STARTS[k]) // 2 for k in HOLDS]
+    place = pick(me, [begin // LANES for begin in begins])
+    offset = pick(me, [begin % LANES for begin in begins])
     lane = lax.broadcasted_iota(jnp.int32, (3, ROWS, LANES), 2)
     left = lane >= offset
 
@@ -258,7 +260,7 @@
 
 
 def main_kernel(
-    n_tm, seg,
+    n_tm,
     live_hbm, nb_hbm, win_ref, out_ref,
     state, mid, delta, ga, ka, send, recv, run, live_ref, nb_ref,
     in_sem, tm_send, tm_recv,
@@ -306,10 +308,13 @@
 
     fine(state, mid)
 
+    lane = lax.broadcasted_iota(jnp.int32, (HALF, LANES), 1)
+    begin = pick(me, [STARTS[k] for k in HOLDS])
+    near = ((lane - begin) & (LANES - 1)) < LANES // 2
+
     def deliver(n, even, odd):
         for f in range(3):
-            send[n, f, pl.ds(0, HALF, stride=2), :] = even[f]
-            send[n, f, pl.ds(1, HALF, stride=2), :] = odd[f]
+            send[n, f] = jnp.where(near, even[f], shift(odd[f], LANES // 2))
 
     def message(n):
         return pltpu.make_async_remote_copy(
@@ -368,14 +373,22 @@
             even.append(a + d)
             odd.append(b + d)
             out.append(d + 0.5 * (a + b))
-        deliver(n, even, odd)
-        dispatch(n)
-        return out
+        return out, even, odd
 
     k2, k7 = coarse(mean(0), row), coarse(c7, row)
     for f in range(3):
         ka[n_tm - 1, f] = k7[f]
-    lax.fori_loop(3, n_tm, lambda n, c: keep2(n, coarse(c, row)), keep2(2, k2))
+
+    def chain2(n, carry):
+        c, even, odd = carry
+        k = coarse(c, row)
+        deliver(n - 1, even, odd)
+        dispatch(n - 1)
+        return keep2(n, k)
+
+    _, even, odd = lax.fori_loop(3, n_tm, chain2, keep2(2, k2))
+    deliver(n_tm - 1, even, odd)
+    dispatch(n_tm - 1)
 
     recv[me] = send[me]
     for c in copies:
@@ -389,17 +402,18 @@
                 device_id=(p, own), device_id_type=MESH,
             ).wait()
 
-    lane = lax.broadcasted_iota(jnp.int32, (HALF, LANES), 1)
+    far = (lane + LANES // 2) & (LANES - 1)
     for b in range(blocks):
         lo = LANES * b
-        parts = [p for p in range(n_tm) if seg * p < lo + LANES and seg * p + seg > lo]
-        for f in range(3):
-            for half in range(2):
-                rows = pl.ds(HALF * half, HALF)
-                value = recv[parts[0], f, rows, :]
-                for p in parts[1:]:
-                    value = jnp.where(lane >= seg * p - lo, recv[p, f, rows, :], value)
-                run[b, f, rows, :] = value
+        parts = [k for k in range(n_tm) if STARTS[k] < lo + LANES and STARTS[k + 1] > lo]
+        for f in range(3):
+            even = odd = recv[HOLDS.index(parts[0]), f]
+            for k in parts[1:]:
+                piece = recv[HOLDS.index(k), f]
+                even = jnp.where(lane >= STARTS[k] - lo, piece, even)
+                odd = jnp.where(far >= STARTS[k] - lo, piece, odd)
+            run[b, f, pl.ds(0, HALF, stride=2), :] = even
+            run[b, f, pl.ds(1, HALF, stride=2), :] = shift(odd, LANES // 2)
     for b in range(blocks):
         spot = jnp.int32(0)
         for i in range(1, blocks):
@@ -410,7 +424,7 @@
 def solution(mesh):
     n_tm, owners = mesh.shape["tm"], mesh.shape["space"]
     blocks = 3
-    seg = blocks * LANES // n_tm
+    assert n_tm == len(HOLDS) and STARTS[-1] == blocks * LANES
     f32, i32 = jnp.float32, jnp.int32
     dma = pltpu.SemaphoreType.DMA
     hbm = pl.BlockSpec(memory_space=pltpu.HBM)
@@ -420,7 +434,7 @@
     def local(water_depth, momentum, slot_live, neighbours):
         sides = neighbours.T
         window = pl.pallas_call(
-            functools.partial(window_kernel, n_tm, owners, seg),
+            functools.partial(window_kernel, owners),
             out_shape=pltpu.VMEM((3, ROWS, LANES), f32),
             in_specs=[hbm] * 4,
             out_specs=vmem,
@@ -437,7 +451,7 @@
             name="window",
         )(slot_live, sides, water_depth, momentum)
         return pl.pallas_call(
-            functools.partial(main_kernel, n_tm, seg),
+            functools.partial(main_kernel, n_tm),
             out_shape=pltpu.VMEM((1, blocks, 3, ROWS, LANES), f32),
             in_specs=[hbm, hbm, vmem],
             out_specs=vmem,
@@ -447,8 +461,8 @@
                 pltpu.VMEM((3, HALF * HALF, LANES), f32),
                 pltpu.VMEM((n_tm, 3, HALF, LANES), f32),
                 pltpu.VMEM((n_tm, 3, HALF, LANES), f32),
-                pltpu.VMEM((n_tm, 3, ROWS, LANES), f32),
-                pltpu.VMEM((n_tm, 3, ROWS, LANES), f32),
+                pltpu.VMEM((n_tm, 3, HALF, LANES), f32),
+                pltpu.VMEM((n_tm, 3, HALF, LANES), f32),
                 pltpu.VMEM((blocks, 3, ROWS, LANES), f32),
                 *small,
                 dma((2,)),

time: 21.8 us -> 20.3 us (0.931)
  Pallas kernels: 21 us -> 19.5 us
    pallas_call x2, Pallas kernels: 21 us -> 19.5 us  [the longest x1 10.9 us: local(): pl.pallas_call(functools.partial(window_kernel, owners), out_shape=pltpu....]
where the time goes in v1:
time: 20.3 us; the launch traced here: 20.2 us
  Pallas kernels  19.5 us (96%)
  local copies, waits for them, and re-layouts  0.64 us (3%)
    pallas_call x1, Pallas kernels, local(): pl.pallas_call(functools.partial(window_kernel, owners), out_shape=pltpu....  10.9 us
    pallas_call x1, Pallas kernels, local(): pl.pallas_call(functools.partial(main_kernel, n_tm), out_shape=pltpu.VMEM...  8.58 us
    unnamed x1, local copies, waits for them, and re-layouts  0.64 us

profile of v1, /device:TPU:1, one launch (start us, length us, event | category | flops | bytes accessed | tf_op | source)
XLA Modules:
  0.0 20.2 jit_solution(16683422996827521236)
XLA Ops:
  0.0 10.9 %window.1.win_ref = f32[3,16,128]{2,1,0:T(8,128)S(1)} custom-call(s32[3]{0:T(128)} %live_hbm.3, s32[2,3]{1,0:T(2,128)} %bitcast.1, f32[3,16,128]{2,1,0:T(8,128)} %depth_ref.1, f32[3,2,16,128]{3,2,1,0:T(8,128)} %mom_ref.1), custom_call_target="tpu_custom_call" | custom-call | tf_op jit(solution)/shard_map/window/pallas_call | solution.py:436
  10.9 8.6 %parareal.1 = f32[1,3,3,16,128]{4,3,2,1,0:T(8,128)S(1)} custom-call(s32[3]{0:T(128)} %live_hbm.3, s32[2,3]{1,0:T(2,128)} %bitcast.2, f32[3,16,128]{2,1,0:T(8,128)S(1)} %window.1.win_ref), custom_call_target="tpu_custom_call" | custom-call | tf_op jit(solution)/shard_map/parareal/pallas_call | solution.py:453
  19.5 0.6 %copy.6 = f32[1,3,3,16,128]{4,3,2,1,0:T(8,128)} copy(f32[1,3,3,16,128]{4,3,2,1,0:T(8,128)S(1)} %parareal.1) | data formatting | bytes 147456

commit v2 on v1

--- a/solution.py
+++ b/solution.py
@@ -92,19 +92,17 @@
     ]
 
 
-def fine_pass(load, emit, ahead=2):
+def fine_pass(load, emit, ahead=3):
     v, d, e, w = {}, {}, {}, {}
     low = None
     for t in range(ROWS + 2 * ahead):
         if t < ROWS:
             v[t] = load(t)
             d[t] = derived(*v[t])
-            e[t] = [shift(x, 1) for x in (*v[t], d[t][0], d[t][1], d[t][3])]
+            e[t] = [shift(x, 1) for x in v[t]]
         j = t - ahead
         if 0 <= j < ROWS:
-            f1, f2, g2, sx, sy = d[j]
-            x = e[j]
-            wx = faces(v[j], x[:3], (v[j][1], f1, f2), (x[1], x[3], x[4]), sx, x[5])
+            wx = lane_face(v[j], d[j], e[j], derived(*e[j]))
             w[j] = (wx, [shift(y, -1) for y in wx])
         j = t - 2 * ahead
         if 0 <= j < ROWS:

time: 20.3 us -> 19.3 us (0.951)
  Pallas kernels: 19.5 us -> 18.5 us
    pallas_call x1, Pallas kernels: 8.58 us -> 7.55 us  [local(): pl.pallas_call(functools.partial(main_kernel, n_tm), out_shape=pltpu.VMEM...]
where the time goes in v2:
time: 19.3 us; the launch traced here: 19.1 us
  Pallas kernels  18.5 us (96%)
  local copies, waits for them, and re-layouts  0.64 us (3%)
    pallas_call x1, Pallas kernels, local(): pl.pallas_call(functools.partial(window_kernel, owners), out_shape=pltpu....  10.9 us
    pallas_call x1, Pallas kernels, local(): pl.pallas_call(functools.partial(main_kernel, n_tm), out_shape=pltpu.VMEM...  7.55 us
    unnamed x1, local copies, waits for them, and re-layouts  0.64 us

profile of v2, /device:TPU:1, one launch (start us, length us, event | category | flops | bytes accessed | tf_op | source)
XLA Modules:
  0.0 19.1 jit_solution(15919947244030568707)
XLA Ops:
  0.0 10.9 %window.1.win_ref = f32[3,16,128]{2,1,0:T(8,128)S(1)} custom-call(s32[3]{0:T(128)} %live_hbm.3, s32[2,3]{1,0:T(2,128)} %bitcast.1, f32[3,16,128]{2,1,0:T(8,128)} %depth_ref.1, f32[3,2,16,128]{3,2,1,0:T(8,128)} %mom_ref.1), custom_call_target="tpu_custom_call" | custom-call | tf_op jit(solution)/shard_map/window/pallas_call | solution.py:434
  10.9 7.5 %parareal.1 = f32[1,3,3,16,128]{4,3,2,1,0:T(8,128)S(1)} custom-call(s32[3]{0:T(128)} %live_hbm.3, s32[2,3]{1,0:T(2,128)} %bitcast.2, f32[3,16,128]{2,1,0:T(8,128)S(1)} %window.1.win_ref), custom_call_target="tpu_custom_call" | custom-call | tf_op jit(solution)/shard_map/parareal/pallas_call | solution.py:451
  18.5 0.6 %copy.6 = f32[1,3,3,16,128]{4,3,2,1,0:T(8,128)} copy(f32[1,3,3,16,128]{4,3,2,1,0:T(8,128)S(1)} %parareal.1) | data formatting | bytes 147456

commit v3 on v2

--- a/solution.py
+++ b/solution.py
@@ -220,9 +220,11 @@
         for o in (west_owner, east_owner):
             pl.semaphore_signal(barrier, inc=1, device_id=(me, o), device_id_type=MESH)
 
-    for c in copies:
+    for c in copies[:2]:
         c.wait()
     lives, count, final, order = tables(live_ref, nb_ref, blocks)
+    for c in copies[2:]:
+        c.wait()
 
     halo = pltpu.make_async_remote_copy(
         src_ref=edge, dst_ref=got, send_sem=edge_send, recv_sem=edge_recv,
@@ -302,7 +304,9 @@
             state[f, pl.ds(n + 9, HALF, stride=16), :] = g[f]
         return g
 
-    c6 = lax.fori_loop(0, n_tm - 2, chain0, mean(0))
+    c6 = mean(0)
+    for n in range(n_tm - 2):
+        c6 = chain0(n, c6)
 
     fine(state, mid)
 
@@ -351,7 +355,9 @@
     def chain1(n, c):
         return keep1(n, coarse(c, row), [ga[n, f] for f in range(3)])
 
-    c7 = lax.fori_loop(2, n_tm - 1, chain1, c)
+    c7 = c
+    for n in range(2, n_tm - 1):
+        c7 = chain1(n, c7)
     for f in range(3):
         for j in range(HALF):
             d = delta[f, HALF * j : HALF * j + HALF, :]
@@ -392,13 +398,16 @@
     for c in copies:
         c.wait()
     lives, count, _, order = tables(live_ref, nb_ref, blocks)
-    for p in range(n_tm):
+    def other(p):
+        return pltpu.make_async_remote_copy(
+            src_ref=send.at[p], dst_ref=recv.at[p], send_sem=tm_send.at[p], recv_sem=tm_recv.at[p],
+            device_id=(p, own), device_id_type=MESH,
+        )
+
+    for p in sorted(range(n_tm), key=lambda n: n % 2):
         @pl.when(p != me)
         def _():
-            pltpu.make_async_remote_copy(
-                src_ref=send.at[p], dst_ref=recv.at[p], send_sem=tm_send.at[p], recv_sem=tm_recv.at[p],
-                device_id=(p, own), device_id_type=MESH,
-            ).wait()
+            other(p).wait_recv()
 
     far = (lane + LANES // 2) & (LANES - 1)
     for b in range(blocks):
@@ -417,6 +426,10 @@
         for i in range(1, blocks):
             spot = jnp.where(jnp.logical_and(order[i] == b, count > i), i, spot)
         out_ref[0, b] = jnp.where(lives[b], run[spot], 0.0)
+    for p in range(n_tm):
+        @pl.when(p != me)
+        def _():
+            other(p).wait_send()
 
 
 def solution(mesh):

time: 19.3 us -> 19.2 us (level)
  no operation moved by 1% of the time
where the time goes in v3:
time: 19.2 us; the launch traced here: 19 us
  Pallas kernels  18.4 us (96%)
  local copies, waits for them, and re-layouts  0.64 us (3%)
    pallas_call x1, Pallas kernels, local(): pl.pallas_call(functools.partial(window_kernel, owners), out_shape=pltpu....  10.9 us
    pallas_call x1, Pallas kernels, local(): pl.pallas_call(functools.partial(main_kernel, n_tm), out_shape=pltpu.VMEM...  7.46 us
    unnamed x1, local copies, waits for them, and re-layouts  0.64 us

profile of v3, /device:TPU:1, one launch (start us, length us, event | category | flops | bytes accessed | tf_op | source)
XLA Modules:
  0.0 19.0 jit_solution(738074991740468685)
XLA Ops:
  0.0 10.9 %window.1.win_ref = f32[3,16,128]{2,1,0:T(8,128)S(1)} custom-call(s32[3]{0:T(128)} %live_hbm.3, s32[2,3]{1,0:T(2,128)} %bitcast.1, f32[3,16,128]{2,1,0:T(8,128)} %depth_ref.1, f32[3,2,16,128]{3,2,1,0:T(8,128)} %mom_ref.1), custom_call_target="tpu_custom_call" | custom-call | tf_op jit(solution)/shard_map/window/pallas_call | solution.py:447
  10.9 7.5 %parareal.1 = f32[1,3,3,16,128]{4,3,2,1,0:T(8,128)S(1)} custom-call(s32[3]{0:T(128)} %live_hbm.3, s32[2,3]{1,0:T(2,128)} %bitcast.2, f32[3,16,128]{2,1,0:T(8,128)S(1)} %window.1.win_ref), custom_call_target="tpu_custom_call" | custom-call | tf_op jit(solution)/shard_map/parareal/pallas_call | solution.py:464
  18.4 0.6 %copy.6 = f32[1,3,3,16,128]{4,3,2,1,0:T(8,128)} copy(f32[1,3,3,16,128]{4,3,2,1,0:T(8,128)S(1)} %parareal.1) | data formatting | bytes 147456
